TPU v7x, 32 devices: a whole 2x2x4 slice. The times are simulated.
32 devices in a mesh: grp: 2 (over y), ka: 4 (over z), ga: 2 (over x), ba: 2 (over core).
Axes of the slice: x: 2, y: 2, z: 4, core: 2. Of those that a mesh axis runs over, the one named last changes fastest.
Arguments:
- coefficients: bfloat16 [2, 2, 16, 512, 9216], P(None, None, ('grp', 'ka'), 'ba', 'ga'), parts along dimension 2, may hold values from -1 to 1
- occupied: int32 [2, 16], P(None, ('grp', 'ka')), parts along dimension 1, may hold values from 64 to 512
- kweights: float32 [16], P(('grp', 'ka')), parts along dimension 0, may hold values from 0.5 to 2
- owner_map: int32 [1024], P('grp'), parts along dimension 0, may hold values from 0 to 7, as said below
- species: int32 [1024], P('grp'), parts along dimension 0, may hold values from 0 to 1
- positions: float32 [3, 1024], P(None, 'grp'), parts along dimension 1, may hold values from 0 to 100
- multipole: float32 [2, 9, 324], replicated, may hold values from -0.3125 to 0.3125
- widths: float32 [2], replicated, may hold values from 0.05 to 0.3
- potential: float32 [2, 442368], P(None, ('grp', 'ga')), parts along dimension 1, may hold values from -0.013671875 to 0.013671875
Outputs:
- density: float32 [2, 2, 1024, 324], P(None, None, ('grp', 'ka', 'ga', 'ba')), parts along dimension 2
- forces: float32 [3, 1024], P(None, ('grp', 'ka', 'ga', 'ba')), parts along dimension 1
There are 2 independent parts, one for each index of `grp`. A program takes and returns all parts, laid end to end along the dimension named above; an argument that names none is the same for every part. Nothing has to cross between parts.
Inputs may be any that keep to these rules, and one draw needn't show every extreme that they name: `owner_map`: within each aligned block of 256 atoms every owner number is named by exactly 32 atoms.
All inputs are finite; a program needn't handle non-finite values.
Results may differ from a plain program's by a relative error of at most 0.0003.
Values sent between devices are 32-bit elements; how exact they have to be, the bound alone decides.
A program may use at most 192 MiB of HBM per device.

v0:
```python
import functools
import math

import jax
import jax.numpy as jnp
import numpy as np
from jax import lax
from jax.experimental import pallas as pl
from jax.experimental.pallas import tpu as pltpu
from jax.sharding import PartitionSpec as P

NPROJ = 18
SPECIES = 2
NL = 9
GRID = 96
LANES = 128

grid_step = 0.0625
highest = lax.Precision.HIGHEST


def group_width():
    return NPROJ * LANES // math.gcd(NPROJ, LANES)


@functools.lru_cache(None)
def gram_tables():
    tiles = group_width() // LANES
    lane = np.arange(LANES)
    same, pick = [], []
    for t in range(tiles):
        rows = t * LANES + lane
        other = np.where(lane < LANES // 2, (t + 1) * LANES + lane, (t - 1) * LANES + lane)
        cols = np.concatenate([rows, other])
        same.append(rows[:, None] // NPROJ == cols[None, :] // NPROJ)
        pick.append(cols[:, None] % NPROJ == lane[None, :])
    return np.stack(same).astype(np.float32), np.stack(pick).astype(np.float32)


@functools.lru_cache(None)
def monomials():
    powers = [
        (i, j, k) for i in range(4) for j in range(4 - i) for k in range(4 - i - j)
    ]
    shapes = [
        {(0, 0, 0): 1.0},
        {(1, 0, 0): 1.0},
        {(0, 1, 0): 1.0},
        {(0, 0, 1): 1.0},
        {(1, 1, 0): 1.0},
        {(0, 1, 1): 1.0},
        {(1, 0, 1): 1.0},
        {(2, 0, 0): 1.0, (0, 2, 0): -1.0},
        {(0, 0, 2): 2.0, (2, 0, 0): -1.0, (0, 2, 0): -1.0},
    ]
    table = np.zeros((4, 16, 3, NL), np.float32)
    for c in range(3):
        for l, terms in enumerate(shapes):
            for power, value in terms.items():
                i, j, k = (p + (axis == c) for axis, p in enumerate(power))
                table[i, j * 4 + k, c, l] += value
    return table


def gram_kernel(occ_ref, weight_ref, x_ref, same_ref, pick_ref, out_ref, rows_ref):
    spin = pl.program_id(0)
    kcount, bcount, width = x_ref.shape[2:]
    tiles = width // LANES
    atoms = width // NPROJ
    band = lax.broadcasted_iota(jnp.int32, (bcount, LANES), 0)
    masks = [
        (band < occ_ref[spin, k]).astype(jnp.float32).astype(jnp.bfloat16)
        for k in range(kcount)
    ]
    low = lax.broadcasted_iota(jnp.int32, (bcount, LANES), 1) < LANES // 2
    for t in range(tiles):
        here = slice(t * LANES, (t + 1) * LANES)
        before = slice(max(t - 1, 0) * LANES, max(t - 1, 0) * LANES + LANES)
        after = slice(min(t + 1, tiles - 1) * LANES, min(t + 1, tiles - 1) * LANES + LANES)
        real, imag = None, None
        for k in range(kcount):
            windows, turned = [], []
            for c in range(2):
                own = x_ref[0, c, k, :, here]
                other = jnp.where(low, x_ref[0, c, k, :, after], x_ref[0, c, k, :, before])
                windows.append(jnp.concatenate([own * masks[k], other * masks[k]], axis=1))
                turned.append(own.T)

            def dot(a, b):
                return jnp.dot(turned[a], windows[b], preferred_element_type=jnp.float32)

            weight = weight_ref[k]
            re = (dot(0, 0) + dot(1, 1)) * weight
            im = (dot(0, 1) - dot(1, 0)) * weight
            real = re if real is None else real + re
            imag = im if imag is None else imag + im
        pick = pick_ref[t]
        for c, value in enumerate((real, imag)):
            value = value * same_ref[t].astype(jnp.float32)
            high = value.astype(jnp.bfloat16)
            rest = (value - high.astype(jnp.float32)).astype(jnp.bfloat16)
            rows_ref[c, here, :] = jnp.dot(
                high, pick, preferred_element_type=jnp.float32
            ) + jnp.dot(rest, pick, preferred_element_type=jnp.float32)
    lane = lax.broadcasted_iota(jnp.int32, (atoms, LANES), 1)
    for c in range(2):
        sums = [None] * (out_ref.shape[3] // LANES)
        for i in range(NPROJ):
            piece = rows_ref[c, pl.ds(i, atoms, stride=NPROJ), :]
            at, offset = divmod(i * NPROJ, LANES)
            if offset:
                piece = pltpu.roll(piece, offset, 1)
            parts = [(at, piece)]
            if offset + NPROJ > LANES:
                parts = [
                    (at, jnp.where(lane >= offset, piece, 0.0)),
                    (at + 1, jnp.where(lane >= offset, 0.0, piece)),
                ]
            for tile, part in parts:
                sums[tile] = part if sums[tile] is None else sums[tile] + part
        for tile, total in enumerate(sums):
            out_ref[0, c, :, tile * LANES : (tile + 1) * LANES] = total


def gram(coefficients, held, kweights):
    spins, parts, kcount, bcount, columns = coefficients.shape
    width = group_width()
    groups = columns // width
    atoms = width // NPROJ
    padded = -(-NPROJ * NPROJ // LANES) * LANES
    same, pick = gram_tables()
    tiles = width // LANES
    return pl.pallas_call(
        gram_kernel,
        grid=(spins, groups),
        out_shape=jax.ShapeDtypeStruct((spins, parts, columns // NPROJ, padded), jnp.float32),
        in_specs=[
            pl.BlockSpec(memory_space=pltpu.SMEM),
            pl.BlockSpec(memory_space=pltpu.SMEM),
            pl.BlockSpec((1, parts, kcount, bcount, width), lambda s, g: (s, 0, 0, 0, g)),
            pl.BlockSpec((tiles, LANES, 2 * LANES), lambda s, g: (0, 0, 0)),
            pl.BlockSpec((tiles, 2 * LANES, LANES), lambda s, g: (0, 0, 0)),
        ],
        out_specs=pl.BlockSpec((1, parts, atoms, padded), lambda s, g: (s, 0, g, 0)),
        scratch_shapes=[pltpu.VMEM((parts, width, LANES), jnp.float32)],
        compiler_params=pltpu.CompilerParams(
            dimension_semantics=("arbitrary", "arbitrary"), vmem_limit_bytes=40 * 2**20
        ),
        cost_estimate=pl.CostEstimate(
            flops=16 * spins * kcount * bcount * columns * 2 * LANES,
            bytes_accessed=coefficients.size * 2,
            transcendentals=0,
        ),
    )(held, kweights, coefficients, jnp.asarray(same, jnp.bfloat16), jnp.asarray(pick, jnp.bfloat16))


def gather_kernel(
    rows_ref, terms_ref, total_ref, sum_ref, first, held, second, third,
    send1, recv1, send2, recv2, send3, recv3,
):
    mesh_id = pl.DeviceIdType.MESH
    ka, ba, ga = (lax.axis_size(name) for name in ("ka", "ba", "ga"))
    k, b, g = (lax.axis_index(name) for name in ("ka", "ba", "ga"))
    barrier = pltpu.get_barrier_semaphore()
    for name, me, size in (("ka", k, ka), ("ba", b, ba), ("ga", g, ga)):
        for step in range(1, size):
            pl.semaphore_signal(
                barrier, inc=1, device_id={name: lax.rem(me + step, size)}, device_id_type=mesh_id
            )
    pl.semaphore_wait(barrier, ka + ba + ga - 3)

    copies1, copies2, copies3 = {}, {}, {}
    for turn in list(range(1, ka)) + [0]:
        to = lax.rem(k + turn, ka)
        for step in range(1, ba):
            peer = lax.rem(b + step, ba)
            copy = pltpu.make_async_remote_copy(
                src_ref=rows_ref.at[to, peer],
                dst_ref=first.at[step - 1, turn],
                send_sem=send1.at[step - 1, turn],
                recv_sem=recv1.at[step - 1, turn],
                device_id={"ba": peer},
                device_id_type=mesh_id,
            )
            copy.start()
            copies1[turn, step] = copy
    for step in range(1, ga):
        peer = lax.rem(g + step, ga)
        copy = pltpu.make_async_remote_copy(
            src_ref=terms_ref.at[peer],
            dst_ref=third.at[step - 1],
            send_sem=send3.at[step - 1],
            recv_sem=recv3.at[step - 1],
            device_id={"ga": peer},
            device_id_type=mesh_id,
        )
        copy.start()
        copies3[step] = copy
    for turn in range(1, ka):
        to = lax.rem(k + turn, ka)
        value = rows_ref[to, b]
        for step in range(1, ba):
            copies1[turn, step].wait_recv()
            value = value + first[step - 1, turn]
        held[turn - 1] = value
        copy = pltpu.make_async_remote_copy(
            src_ref=held.at[turn - 1],
            dst_ref=second.at[turn - 1],
            send_sem=send2.at[turn - 1],
            recv_sem=recv2.at[turn - 1],
            device_id={"ka": to},
            device_id_type=mesh_id,
        )
        copy.start()
        copies2[turn] = copy
    value = rows_ref[k, b]
    for step in range(1, ba):
        copies1[0, step].wait_recv()
        value = value + first[step - 1, 0]
    terms = terms_ref[g]
    for step in range(1, ga):
        copies3[step].wait_recv()
        terms = terms + third[step - 1]
    sum_ref[...] = terms
    for turn in range(1, ka):
        copies2[turn].wait_recv()
        value = value + second[turn - 1]
    total_ref[...] = value
    for copy in [*copies1.values(), *copies2.values(), *copies3.values()]:
        copy.wait_send()


def gather_sums(rows, terms):
    ka, ba = rows.shape[:2]
    chunk, piece = rows.shape[2:], terms.shape[1:]
    ga = lax.axis_size("ga")
    vmem = pl.BlockSpec(memory_space=pltpu.VMEM)
    return pl.pallas_call(
        gather_kernel,
        out_shape=(
            jax.ShapeDtypeStruct(chunk, jnp.float32),
            jax.ShapeDtypeStruct(piece, jnp.float32),
        ),
        in_specs=[vmem, vmem],
        out_specs=(vmem, vmem),
        scratch_shapes=[
            pltpu.VMEM((ba - 1, ka, *chunk), jnp.float32),
            pltpu.VMEM((ka - 1, *chunk), jnp.float32),
            pltpu.VMEM((ka - 1, *chunk), jnp.float32),
            pltpu.VMEM((ga - 1, *piece), jnp.float32),
            pltpu.SemaphoreType.DMA((ba - 1, ka)),
            pltpu.SemaphoreType.DMA((ba - 1, ka)),
            pltpu.SemaphoreType.DMA((ka - 1,)),
            pltpu.SemaphoreType.DMA((ka - 1,)),
            pltpu.SemaphoreType.DMA((ga - 1,)),
            pltpu.SemaphoreType.DMA((ga - 1,)),
        ],
        compiler_params=pltpu.CompilerParams(collective_id=0, has_side_effects=True),
    )(rows, terms)


def signed_steps(index):
    return grid_step * jnp.where(index >= GRID // 2, index - GRID, index).astype(jnp.float32)


def wave_sums(places, spread, potential, first_plane):
    atoms = places.shape[1]
    planes = potential.shape[1] // (GRID * GRID)
    line = signed_steps(jnp.arange(GRID, dtype=jnp.int32))
    depth = signed_steps(first_plane + jnp.arange(planes, dtype=jnp.int32))

    def factor(axis, steps):
        angle = places[axis][:, None] * steps[None, :]
        damp = jnp.exp(-spread[:, None] * (steps * steps)[None, :])
        return damp * jnp.cos(angle), damp * jnp.sin(angle)

    cos_x, sin_x = factor(0, line)
    cos_y, sin_y = factor(1, line)
    cos_z, sin_z = factor(2, depth)
    power_x = jnp.stack([jnp.ones_like(line), line, line * line, line * line * line])
    left = jnp.stack(
        [
            jnp.concatenate([cos_x, sin_x], axis=1),
            jnp.concatenate([sin_x, -cos_x], axis=1),
        ]
    )
    left = left[:, None] * jnp.concatenate([power_x, power_x], axis=1)[None, :, None, :]
    grid = potential.reshape(2, planes * GRID, GRID)
    right = jnp.concatenate([grid[1], grid[0]], axis=1)
    along = lax.dot_general(
        left.reshape(8 * atoms, 2 * GRID), right, (((1,), (1,)), ((), ())), precision=highest
    ).reshape(2, 4, atoms, planes, GRID)
    cos_yz = cos_z[:, :, None] * cos_y[:, None, :] - sin_z[:, :, None] * sin_y[:, None, :]
    sin_yz = cos_z[:, :, None] * sin_y[:, None, :] + sin_z[:, :, None] * cos_y[:, None, :]
    wave = along[0] * cos_yz[None] - along[1] * sin_yz[None]
    power_z = jnp.stack([jnp.ones_like(depth), depth, depth * depth, depth * depth * depth])
    weights = power_z[None, :, :, None] * power_x[:, None, None, :]
    sums = jnp.dot(
        wave.reshape(4 * atoms, planes * GRID),
        weights.reshape(16, planes * GRID).T,
        precision=highest,
    ).reshape(4, atoms, 16)
    return jnp.einsum("ian,incl->acl", sums, jnp.asarray(monomials()), precision=highest)


def shards(
    coefficients, occupied, kweights, owner_map, species, positions, multipole, widths, potential
):
    spins, parts, kcount, bcount, columns = coefficients.shape
    atoms_blk = columns // NPROJ
    owners = lax.axis_size("ka") * lax.axis_size("ba")
    per_owner = atoms_blk // owners
    owner_index = lax.axis_index(("ka", "ba"))
    group_index = lax.axis_index("ga")
    held = occupied - lax.axis_index("ba") * bcount
    density_local = gram(coefficients, held, kweights)

    owner_rows = owner_map.reshape(-1, atoms_blk)
    blocks = owner_rows.shape[0]
    number = jnp.arange(atoms_blk, dtype=jnp.int32)
    ahead = (owner_rows[:, None, :] == owner_rows[:, :, None]) & (
        number[None, None, :] < number[None, :, None]
    )
    spot = owner_rows * per_owner + jnp.sum(ahead.astype(jnp.int32), axis=2)
    my_spot = lax.dynamic_index_in_dim(spot, group_index, 0, keepdims=False)
    route = (number[:, None] == my_spot[None, :]).astype(jnp.float32)
    routed = jnp.einsum(
        "opa,scae->oscpe", route.reshape(owners, per_owner, atoms_blk), density_local, precision=highest
    )
    mine = owner_index * per_owner + jnp.arange(per_owner, dtype=jnp.int32)
    chosen = spot[:, None, :] == mine[None, :, None]
    places = jnp.sum(
        jnp.where(chosen[None], positions.reshape(3, blocks, 1, atoms_blk), 0.0), axis=3
    ).reshape(3, -1)
    kinds = jnp.sum(jnp.where(chosen, species.reshape(blocks, 1, atoms_blk), 0), axis=2)
    spread = jnp.where(kinds.reshape(-1) == 0, widths[0], widths[1])
    first_plane = group_index * (potential.shape[1] // (GRID * GRID))
    terms = wave_sums(places, spread, potential, first_plane)
    terms = terms.reshape(blocks, per_owner, 3 * NL)
    terms = jnp.pad(terms, ((0, 0), (0, 0), (0, -3 * NL % LANES)))
    rows = routed.reshape(
        lax.axis_size("ka"), lax.axis_size("ba"), spins * parts, per_owner, routed.shape[-1]
    )
    total, own_terms = gather_sums(rows, terms)
    own_density = total.reshape(spins, parts, per_owner, -1)[..., : NPROJ * NPROJ]
    own_terms = own_terms[:, : 3 * NL]
    own_kinds = lax.dynamic_index_in_dim(kinds, group_index, 0, keepdims=False)

    real_total = jnp.sum(own_density[:, 0], axis=0)
    moments = jnp.dot(
        real_total, multipole.reshape(SPECIES * NL, NPROJ * NPROJ).T, precision=highest
    ).reshape(per_owner, SPECIES, NL)
    picked = own_kinds[:, None] == jnp.arange(SPECIES, dtype=jnp.int32)[None, :]
    own_moments = jnp.sum(jnp.where(picked[:, :, None], moments, 0.0), axis=1)
    own_force = jnp.sum(own_terms.reshape(per_owner, 3, NL) * own_moments[:, None, :], axis=2)
    return (own_density, own_force.T)


def solution(mesh):
    placed = (
        P(None, None, ("grp", "ka"), "ba", "ga"),
        P(None, ("grp", "ka")),
        P(("grp", "ka")),
        P("grp"),
        P("grp"),
        P(None, "grp"),
        P(),
        P(),
        P(None, ("grp", "ga")),
    )
    return jax.shard_map(
        shards,
        mesh=mesh,
        in_specs=placed,
        out_specs=(
            P(None, None, ("grp", "ka", "ga", "ba"), None),
            P(None, ("grp", "ka", "ga", "ba")),
        ),
        check_vma=False,
    )
```

profile of v0, /device:TPU:15, one launch (start us, length us, event | category | flops | bytes accessed | tf_op | source)
XLA Modules:
  0.0 94.0 jit_solution(7042963950691802397)
XLA Ops:
  0.7 0.8 reshape.448
  1.5 0.2 convert_reduce_fusion
  1.7 0.7 broadcast_in_dim.52
  2.4 0.2 select_reduce_fusion.1
  2.6 1.3 %fusion.40 = (f32[1]{0:T(128)}, f32[1]{0:T(128)}) fusion(f32[2]{0:T(128)} %param.19), kind=kLoop, calls=%fused_computation.83 | loop fusion | bytes 16 | tf_op jit(solution)/shard_map/slice | solution.py:336
  3.9 1.3 %fusion.24 = f32[2,32]{1,0:T(2,128)S(1)} fusion(s32[2,32]{1,0:T(2,128)S(1)} %select_reduce_fusion.1, f32[]{:T(128)} %bitcast.8, f32[]{:T(128)} %bitcast.7), kind=kLoop, calls=%fused_computation.61 | loop fusion | flops 192 | bytes 520 | tf_op jit(solution)/shard_map/neg | solution.py:274
  5.4 0.7 broadcast_in_dim.58
  6.2 0.6 fusion.39
  7.0 0.9 fusion.17
  8.2 2.4 %slice_reduce_fusion.1 = (f32[110592]{0:T(1024)S(1)}, f32[110592]{0:T(1024)S(1)}) fusion(f32[2,110592]{1,0:T(2,128)S(1)} %copy-done.4), kind=kLoop, calls=%fused_computation.18 | loop fusion | bytes 1769472 | tf_op jit(solution)/shard_map/slice | solution.py:289
  10.6 0.2 squeeze.21
  10.8 1.0 %squeeze.22 = f32[1152,96]{1,0:T(8,128)} reshape(f32[110592]{0:T(1024)S(1)} %get-tuple-element.7) | data formatting | bytes 884736 | tf_op jit(solution)/shard_map/squeeze | solution.py:289
  11.8 3.6 %fusion.6 = f32[512,1152]{1,0:T(8,128)S(1)} fusion(f32[512,192]{1,0:T(8,128)S(1)} %bitcast.50, f32[1152,96]{1,0:T(8,128)} %squeeze.22, f32[1152,96]{1,0:T(8,128)S(1)} %squeeze.21), kind=kOutput, calls=%fused_computation.6 | convolution fusion | flops 1359175680 | bytes 3637248 | tf_op jit(solution)/shard_map/dot_general | solution.py:290
  15.4 0.8 mul.441
  16.4 1.1 %multiply_subtract_fusion = (f32[64,12,96]{2,1,0:T(8,128)S(1)}, f32[64,12,96]{2,1,0:T(8,128)S(1)}) fusion(f32[64,96]{1,0:T(8,128)S(1)} %get-tuple-element.22, f32[64,12]{1,0:T(8,128)S(1)} %copy.27, f32[64,96]{1,0:T(8,128)} %get-tuple-element.23, f32[64,12]{1,0:T(8,128)S(1)} %copy.26), kind=kLoop, calls=%fused_computation.15 | loop fusion | flops 442368 | bytes 645120 | tf_op jit(solution)/shard_map/sub | solution.py:293
  17.6 1.5 %mul.458 = f32[4,64,12,96]{3,2,1,0:T(8,128)} broadcast(f32[64,12,96]{2,1,0:T(8,128)S(1)} %get-tuple-element.8), dimensions={1,2,3} | broadcast | bytes 1474560 | tf_op jit(solution)/shard_map/mul | solution.py:295
  19.1 2.9 %mul.459 = f32[256,1152]{1,0:T(8,128)} reshape(f32[4,64,12,96]{3,2,1,0:T(8,128)} %mul.458) | data formatting | bytes 2359296 | tf_op jit(solution)/shard_map/mul | solution.py:295
  22.0 1.5 %mul.463 = f32[4,64,12,96]{3,2,1,0:T(8,128)} broadcast(f32[64,12,96]{2,1,0:T(8,128)S(1)} %get-tuple-element.9), dimensions={1,2,3} | broadcast | bytes 1474560 | tf_op jit(solution)/shard_map/mul | solution.py:295
  23.5 2.9 %mul.464 = f32[256,1152]{1,0:T(8,128)} reshape(f32[4,64,12,96]{3,2,1,0:T(8,128)} %mul.463) | data formatting | bytes 2359296 | tf_op jit(solution)/shard_map/mul | solution.py:295
  26.3 3.1 %fusion.5 = f32[256,1152]{1,0:T(8,128)} fusion(f32[256,1152]{1,0:T(8,128)} %mul.464, f32[512,1152]{1,0:T(8,128)S(1)} %fusion.6, f32[256,1152]{1,0:T(8,128)} %mul.459), kind=kLoop, calls=%fused_computation.4 | loop fusion | flops 884736 | bytes 5898240 | tf_op jit(solution)/shard_map/sub | solution.py:295
  29.7 3.0 %convolution_bitcast_fusion = f32[4,64,16,1]{1,2,0,3:T(8,128)S(1)} fusion(f32[4,64,1152]{2,1,0:T(8,128)} %bitcast.49, f32[16,1152,1]{1,0,2:T(8,128)S(1)} %reshape.455), kind=kOutput, calls=%fused_computation.10 | convolution fusion | flops 56623104 | bytes 1269760 | tf_op jit(solution)/shard_map/dot_general | solution.py:298
  32.8 0.3 convolution_bitcast_fusion.1
  33.2 0.6 pad.4.terms_ref
  33.9 28.7 %shard_map.131 = f32[2,2,256,384]{3,2,1,0:T(8,128)S(1)} custom-call(s32[2,2]{1,0:T(2,128)S(1)} %broadcast_subtract_fusion.occ_ref, f32[2]{0:T(128)S(1)} %copy-done.1, bf16[2,2,2,256,4608]{4,3,2,1,0:T(8,128)(2,1)} %x_ref.1, bf16[9,128,256]{2,1,0:T(8,128)(2,1)S(1)} %copy-done.2, bf16[9,256,128]{2,1,0:T(8,128)(2,1)S(1)} %copy-done.3), custom_call_target="tpu_custom_call" | custom-call | flops 19327352832 | bytes 18874368 | tf_op jit(solution)/shard_map/pallas_call | solution.py:133
  62.6 1.0 %fusion.2 = f32[8,2,2,32,384]{4,3,0,2,1:T(8,128)S(1)} fusion(f32[2,2,256,384]{3,2,1,0:T(8,128)S(1)} %shard_map.131, s32[256]{0:T(256)S(1)} %bitcast.54, s32[8,32]{1,0:T(8,128)S(1)} %multiply_add_fusion.1), kind=kOutput, calls=%fused_computation.2 | convolution fusion | flops 1208025088 | bytes 3147776 | tf_op jit(solution)/shard_map/opa,scae->oscpe/dot_general | solution.py:327
  63.6 1.3 %copy.25 = f32[8,2,2,32,384]{4,3,2,1,0:T(8,128)} copy(f32[8,2,2,32,384]{4,3,0,2,1:T(8,128)S(1)} %fusion.2) | data formatting | bytes 3145728 | tf_op jit(solution)/shard_map/opa,scae->oscpe/transpose | solution.py:327
  64.9 24.8 %shard_map.132 = (f32[4,32,384]{2,1,0:T(8,128)}, f32[32,128]{1,0:T(8,128)}) custom-call(f32[4,2,4,32,384]{4,3,2,1,0:T(8,128)} %bitcast.48, f32[2,32,128]{2,1,0:T(8,128)} %pad.4.terms_ref), custom_call_target="tpu_custom_call" | custom-call | tf_op jit(solution)/shard_map/pallas_call | solution.py:238
  89.8 0.9 slice_reduce_fusion.2
  90.7 0.2 fusion.10
  90.9 0.8 copy.29
  91.7 0.6 multiply_reduce_fusion
  92.3 1.6 %copy.37 = f32[2,2,32,324]{3,2,1,0:T(8,128)} copy(f32[2,2,32,324]{3,2,1,0:T(8,128)} %bitcast.52) | data formatting | bytes 331776
  (57 shorter events, 1.6 us)
Async XLA Ops:
  0.6 90.1 %copy-start = (f32[2,9,324]{2,0,1:T(2,128)S(1)}, f32[2,9,324]{2,0,1:T(2,128)}, u32[]{:S(2)}) copy-start(f32[2,9,324]{2,0,1:T(2,128)} %param.18) | copy-start | bytes 69988
  0.6 7.6 %copy-start.4 = (f32[2,110592]{1,0:T(2,128)S(1)}, f32[2,110592]{1,0:T(2,128)}, u32[]{:S(2)}) copy-start(f32[2,110592]{1,0:T(2,128)} %param.20) | copy-start | bytes 2654212
  8.0 2.5 %copy-start.6 = (f32[1,96]{1,0:T(1,128)}, f32[1,96]{1,0:T(1,128)S(1)}, u32[]{:S(2)}) copy-start(f32[1,96]{1,0:T(1,128)S(1)} %fusion.34) | copy-start | bytes 1156
  8.1 2.5 %copy-start.8 = (f32[1,96]{1,0:T(1,128)}, f32[1,96]{1,0:T(1,128)S(1)}, u32[]{:S(2)}) copy-start(f32[1,96]{1,0:T(1,128)S(1)} %stack_broadcast_in_dim.3) | copy-start | bytes 1156
  26.3 3.2 %copy-start.7 = (f32[1,96]{1,0:T(1,128)S(1)}, f32[1,96]{1,0:T(1,128)}, u32[]{:S(2)}) copy-start(f32[1,96]{1,0:T(1,128)} %copy-done.6) | copy-start | bytes 1156
  26.3 3.2 %copy-start.9 = (f32[1,96]{1,0:T(1,128)S(1)}, f32[1,96]{1,0:T(1,128)}, u32[]{:S(2)}) copy-start(f32[1,96]{1,0:T(1,128)} %copy-done.8) | copy-start | bytes 1156
  29.4 3.3 %copy-start.5 = (f32[4,16,3,9]{1,3,0,2:T(8,128)S(1)}, f32[4,16,3,9]{1,3,0,2:T(8,128)}, u32[]{:S(2)}) copy-start(f32[4,16,3,9]{1,3,0,2:T(8,128)} %constant.57.clone) | copy-start | bytes 20740
  29.4 4.5 %copy-start.10 = (s32[2,2]{1,0:T(2,128)S(1)}, s32[2,2]{1,0:T(2,128)}, u32[]{:S(2)}) copy-start(s32[2,2]{1,0:T(2,128)} %param.13) | copy-start | bytes 52
  29.4 4.5 %copy-start.1 = (f32[2]{0:T(128)S(1)}, f32[2]{0:T(128)}, u32[]{:S(2)}) copy-start(f32[2]{0:T(128)} %weight_ref.1) | copy-start | bytes 28
  29.4 4.5 %copy-start.2 = (bf16[9,128,256]{2,1,0:T(8,128)(2,1)S(1)}, bf16[9,128,256]{2,1,0:T(8,128)(2,1)}, u32[]{:S(2)}) copy-start(bf16[9,128,256]{2,1,0:T(8,128)(2,1)} %constant.55.clone.same_ref) | copy-start | bytes 1769476
  29.4 4.5 %copy-start.3 = (bf16[9,256,128]{2,1,0:T(8,128)(2,1)S(1)}, bf16[9,256,128]{2,1,0:T(8,128)(2,1)}, u32[]{:S(2)}) copy-start(bf16[9,256,128]{2,1,0:T(8,128)(2,1)} %constant.56.clone.pick_ref) | copy-start | bytes 1769476
where the time goes:
time: 94.6 us; the launch traced here: 94 us
  Pallas kernels  53.6 us (57%)
  local copies, waits for them, and re-layouts  22.2 us (23%)
  other arithmetic  9.16 us (10%)
  matrix products  8.02 us (8%)
  between operations  0.96 us (1%)
    pallas_call x1, Pallas kernels, gram(): pl.pallas_call(gram_kernel, grid=(spins, groups), out_shape=jax.ShapeDtyp...  28.7 us
    pallas_call x1, Pallas kernels, gather_sums(): pl.pallas_call(gather_kernel, out_shape=(jax.ShapeDtypeStruct(chunk, jnp....  24.8 us
    mul x4, local copies, waits for them, and re-layouts, wave_sums(): wave = along[0] * cos_yz[None] - along[1] * sin_yz[None]  8.76 us
    dot_general x1, matrix products, wave_sums(): lax.dot_general(left.reshape(8 * atoms, 2 * GRID), right, (((1,), (1,)),...  3.56 us
    sub x1, other arithmetic, wave_sums(): wave = along[0] * cos_yz[None] - along[1] * sin_yz[None]  3.08 us
    dot_general x1, matrix products, wave_sums(): jnp.dot(wave.reshape(4 * atoms, planes * GRID), weights.reshape(16, plane...  2.99 us
    slice x1, local copies, waits for them, and re-layouts, wave_sums(): right = jnp.concatenate([grid[1], grid[0]], axis=1)  2.35 us

commit v1 on v0

v1 whole, which is shorter than its diff:
```python
import functools
import math

import jax
import jax.numpy as jnp
import numpy as np
from jax import lax
from jax.experimental import pallas as pl
from jax.experimental.pallas import tpu as pltpu
from jax.sharding import PartitionSpec as P

NPROJ = 18
SPECIES = 2
NL = 9
GRID = 96
LANES = 128
SUB = 8
ENTRIES = NPROJ * NPROJ
PAD = -(-ENTRIES // LANES) * LANES
WIN = SUB * NPROJ
SLOTS = 2
HALF = LANES // 2
CHUNK = 3

grid_step = 0.0625
highest = lax.Precision.HIGHEST


def group_width():
    return NPROJ * LANES // math.gcd(NPROJ, LANES)


@functools.lru_cache(None)
def fold_table():
    q = np.zeros((PAD, PAD), np.float32)
    for i in range(NPROJ):
        for j in range(i):
            q[i * NPROJ + j, i * NPROJ + j] += 1.0
            q[j * NPROJ + i, i * NPROJ + j] -= 1.0
    return q


@functools.lru_cache(None)
def open_table():
    u = np.zeros((PAD, 2 * PAD), np.float32)
    for i in range(NPROJ):
        for j in range(NPROJ):
            u[min(i, j) * NPROJ + max(i, j), i * NPROJ + j] = 1.0
            if i > j:
                u[i * NPROJ + j, PAD + i * NPROJ + j] = 1.0
            elif i < j:
                u[j * NPROJ + i, PAD + i * NPROJ + j] = -1.0
    return u


POWERS = [(i, j, k) for i in range(4) for j in range(4 - i) for k in range(4 - i - j)]
SHAPES = [
    {(0, 0, 0): 1.0},
    {(1, 0, 0): 1.0},
    {(0, 1, 0): 1.0},
    {(0, 0, 1): 1.0},
    {(1, 1, 0): 1.0},
    {(0, 1, 1): 1.0},
    {(1, 0, 1): 1.0},
    {(2, 0, 0): 1.0, (0, 2, 0): -1.0},
    {(0, 0, 2): 2.0, (2, 0, 0): -1.0, (0, 2, 0): -1.0},
]
KIND_ROW = len(POWERS)
ROWS = -(-(KIND_ROW + 1) // SUB) * SUB


def split(value):
    high = value.astype(jnp.bfloat16)
    return high, (value - high.astype(jnp.float32)).astype(jnp.bfloat16)


def mdot(a, b):
    return jnp.dot(a, b, preferred_element_type=jnp.float32)


def flags(value):
    return value.astype(jnp.float32).astype(jnp.bfloat16)


def before(count):
    row = lax.broadcasted_iota(jnp.int32, (count, count), 0)
    col = lax.broadcasted_iota(jnp.int32, (count, count), 1)
    return flags(row < col)


def gram_kernel(occ_ref, weight_ref, x_hbm, owner_ref, fold_ref, out_ref, x_ref, xa_ref, xb_ref, sc_ref, t_ref, sems):
    spins, groups, _, kcount, bcount, width = x_ref.shape
    atoms = t_ref.shape[2]
    per = width // NPROJ
    total = spins * groups

    def fetch(n):
        s, g = n // groups, n % groups
        return pltpu.make_async_copy(
            x_hbm.at[s, :, :, :, pl.ds(pl.multiple_of(g*width, width), width)], x_ref.at[s, g], sems.at[s, g])

    for n in range(total):
        fetch(n).start()
    band = lax.broadcasted_iota(jnp.int32, (LANES, bcount), 1) + lax.axis_index("ba") * bcount
    lane = lax.broadcasted_iota(jnp.int32, (SUB, LANES), 1)
    row = lax.broadcasted_iota(jnp.int32, (SUB, LANES), 0)
    shifts = [NPROJ*row + (at*LANES + lane) % NPROJ for at in range(PAD//LANES)]
    past = lax.broadcasted_iota(jnp.int32, (WIN, LANES), 1) - lax.broadcasted_iota(
        jnp.int32, (WIN, LANES), 0) // NPROJ * NPROJ

    def turn(n, xt_ref, t):
        s, g = n // groups, n % groups
        cols = slice(t*LANES, (t+1)*LANES)
        for k in range(kcount):
            mask = (band < occ_ref[s, k]).astype(jnp.float32).astype(jnp.bfloat16)
            for c in range(2):
                v = x_ref[s, g, c, k, :, cols].T * mask
                at = t*LANES
                while at < (t+1)*LANES:
                    w = at // WIN
                    end = min((w+1)*WIN, (t+1)*LANES)
                    xt_ref[k, w, (1-c)*WIN + at - w*WIN:(1-c)*WIN + end - w*WIN, :] = v[at - t*LANES:end - t*LANES]
                    at = end

    def window(n, xt_ref, w):
        s, g = n // groups, n % groups
        base = (w*WIN)//LANES*LANES
        o = w*WIN - base
        win = slice(base, base + 2*LANES)
        take = past < o + NPROJ - LANES
        re = im = None
        for k in range(kcount):
            both = mdot(xt_ref[k, w], x_ref[s, g, 1, k, :, win])
            r = mdot(xt_ref[k, w, WIN:], x_ref[s, g, 0, k, :, win]) + both[:WIN]
            m = both[WIN:]
            weight = weight_ref[k]
            r = jnp.where(take, r[:, LANES:], r[:, :LANES]) * weight
            m = jnp.where(take, m[:, LANES:], m[:, :LANES]) * weight
            re = r if re is None else re + r
            im = m if im is None else im + m
        sc_ref[w % SLOTS, 0] = re
        sc_ref[w % SLOTS, 1] = im

    def unfold(n, w):
        s, g = n // groups, n % groups
        o = w*WIN % LANES
        lifts = [(o + shift) & (LANES - 1) for shift in shifts]
        for c in range(2):
            tiles = [None]*(PAD//LANES)
            for i in range(NPROJ):
                piece = sc_ref[w % SLOTS, c, pl.ds(i, SUB, stride=NPROJ), :]
                for at in range(i*NPROJ // LANES, (i*NPROJ + NPROJ - 1) // LANES + 1):
                    part = jnp.take_along_axis(piece, lifts[at], axis=1, mode="promise_in_bounds")
                    tiles[at] = part if tiles[at] is None else jnp.where(lane >= i*NPROJ - at*LANES, part, tiles[at])
            for at, v in enumerate(tiles):
                here = pl.multiple_of(g*per + w*SUB, SUB)
                t_ref[s, c, pl.ds(here, SUB), at*LANES:(at+1)*LANES] = v

    fetch(0).wait()
    for t in range(width // LANES):
        turn(0, xa_ref, t)

    def step(n, here, there):
        after = jnp.minimum(n + 1, total - 1)
        @pl.when(n + 1 < total)
        def _():
            fetch(n + 1).wait()
        for w in range(width // WIN):
            window(n, here, w)
            turn(after, there, w)
            if w == 0:
                turn(after, there, width // LANES - 1)
            unfold(n, w)

    @pl.loop(0, total // 2)
    def _(pair):
        step(2*pair, xa_ref, xb_ref)
        step(2*pair + 1, xb_ref, xa_ref)

    e = lax.broadcasted_iota(jnp.int32, (atoms, PAD), 1)
    keep = (e // NPROJ <= e % NPROJ) & (e < ENTRIES)
    q = fold_ref[...]
    owners = lax.axis_size("ka") * lax.axis_size("ba")
    owner = owner_ref[:, :atoms]
    for block in range(1, owner_ref.shape[1] // atoms):
        piece = owner_ref[:, block * atoms:(block + 1) * atoms]
        owner = jnp.where(lax.axis_index("ga") == block, piece, owner)
    member = lax.broadcasted_iota(jnp.int32, (max(owners, 2 * SUB), atoms), 0) == owner
    count = mdot(flags(member), before(atoms))
    rank = jnp.sum(jnp.where(member, count, 0.0), axis=0, keepdims=True)
    spot = owner.astype(jnp.float32) * (atoms // owners) + rank
    place = lax.broadcasted_iota(jnp.int32, (atoms, atoms), 0).astype(jnp.float32)
    route = flags(place == spot)
    for s in range(spins):
        hi, lo = split(jnp.where(e < ENTRIES, t_ref[s, 1], 0.0))
        h = jnp.where(keep, t_ref[s, 0], 0.0) + (mdot(hi, q) + mdot(lo, q))
        hi, lo = split(h)
        out_ref[s] = mdot(route, hi) + mdot(route, lo)


def gram(coefficients, occupied, kweights, owner_map):
    spins, parts, kcount, bcount, columns = coefficients.shape
    width = group_width()
    groups = columns // width
    atoms = columns // NPROJ
    vmem = pl.BlockSpec(memory_space=pltpu.VMEM)
    smem = pl.BlockSpec(memory_space=pltpu.SMEM)
    return pl.pallas_call(
        gram_kernel,
        out_shape=jax.ShapeDtypeStruct((spins, atoms, PAD), jnp.float32),
        in_specs=[smem, smem, pl.BlockSpec(memory_space=pl.ANY), vmem, vmem],
        out_specs=vmem,
        scratch_shapes=[
            pltpu.VMEM((spins, groups, parts, kcount, bcount, width), jnp.bfloat16),
            *[pltpu.VMEM((kcount, width // WIN, 2 * WIN, bcount), jnp.bfloat16)] * 2,
            pltpu.VMEM((SLOTS, 2, WIN, LANES), jnp.float32),
            pltpu.VMEM((spins, 2, atoms, PAD), jnp.float32),
            pltpu.SemaphoreType.DMA((spins, groups)),
        ],
        compiler_params=pltpu.CompilerParams(vmem_limit_bytes=48 * 2**20),
    )(occupied, kweights, coefficients, owner_map, jnp.asarray(fold_table(), jnp.bfloat16))


def sincos(angle):
    turns = jnp.floor(angle * (2.0 / math.pi) + 0.5)
    rest = ((angle - turns * 1.5703125) - turns * 4.837512969970703125e-4) - turns * 7.54978995489188216e-8
    z = rest * rest
    sine = ((-1.9515295891e-4 * z + 8.3321608736e-3) * z - 1.6666654611e-1) * z * rest + rest
    cosine = (
        (2.443315711809948e-5 * z - 1.388731625493765e-3) * z + 4.166664568298827e-2
    ) * z * z - 0.5 * z + 1.0
    quarter = turns.astype(jnp.int32) & 3
    odd = (quarter & 1) == 1
    s = jnp.where(odd, cosine, sine)
    c = jnp.where(odd, sine, cosine)
    return jnp.where(quarter >= 2, -s, s), jnp.where((quarter == 1) | (quarter == 2), -c, c)


def signed_steps(index):
    return grid_step * jnp.where(index >= GRID // 2, index - GRID, index).astype(jnp.float32)


def finish_kernel(
    width_ref, rows_ref, owner_ref, kind_ref, place_ref, grid_ref, total_ref, terms_ref,
    first, held, second, sent, third, left_ref, cosy_ref, siny_ref, cosz_ref, sinz_ref,
    send1, recv1, send2, recv2, send3, recv3,
):
    mesh_id = pl.DeviceIdType.MESH
    ka, ba, ga = (lax.axis_size(name) for name in ("ka", "ba", "ga"))
    k, b, g = (lax.axis_index(name) for name in ("ka", "ba", "ga"))
    per = rows_ref.shape[3]
    blocks = ga
    atoms = owner_ref.shape[1] // blocks
    barrier = pltpu.get_barrier_semaphore()
    for name, me, size in (("ka", k, ka), ("ba", b, ba), ("ga", g, ga)):
        for step in range(1, size):
            pl.semaphore_signal(
                barrier, inc=1, device_id={name: lax.rem(me + step, size)}, device_id_type=mesh_id
            )
    pl.semaphore_wait(barrier, ka + ba + ga - 3)

    copies1, copies2, copies3 = {}, {}, {}
    turns = [t // 2 + 1 if t % 2 == 0 else ka - 1 - t // 2 for t in range(ka - 1)][::-1] + [0]
    for turn in turns:
        to = lax.rem(k + turn, ka)
        for step in range(1, ba):
            peer = lax.rem(b + step, ba)
            copy = pltpu.make_async_remote_copy(
                src_ref=rows_ref.at[:, to, peer],
                dst_ref=first.at[step - 1, turn],
                send_sem=send1.at[step - 1, turn],
                recv_sem=recv1.at[step - 1, turn],
                device_id={"ba": peer},
                device_id_type=mesh_id,
            )
            copy.start()
            copies1[turn, step] = copy

    columns = []
    for block in range(blocks):
        span = slice(block * atoms, (block + 1) * atoms)
        mine = owner_ref[:, span] == k * ba + b
        rank = mdot(jnp.broadcast_to(flags(mine), (2 * SUB, atoms)), before(atoms))[:1]
        spot = lax.broadcasted_iota(jnp.int32, (per, atoms), 0).astype(jnp.float32)
        chosen = mine & (rank == spot)
        columns.append([
            jnp.sum(jnp.where(chosen, value, 0.0), axis=1, keepdims=True)
            for value in (
                place_ref[0:1, span], place_ref[1:2, span], place_ref[2:3, span],
                kind_ref[:, span].astype(jnp.float32),
            )
        ])
    lane = lax.broadcasted_iota(jnp.int32, (HALF, LANES), 1)
    table = jnp.zeros((HALF, LANES), jnp.float32)
    spare = HALF - blocks * per
    for at in range(4):
        pieces = [columns[block][at] for block in range(blocks)]
        if spare:
            pieces.append(jnp.zeros((spare, 1), jnp.float32))
        table = jnp.where(lane == at, jnp.concatenate(pieces, axis=0), table)
    flat = jnp.concatenate([table, table], axis=0).T
    kinds = flat[3:4]
    spread = jnp.where(kinds == 0.0, width_ref[0], width_ref[1])

    steps = signed_steps(lax.broadcasted_iota(jnp.int32, (GRID, LANES), 0))
    damp = jnp.exp(-spread * (steps * steps))
    sine, cosine = sincos(flat[0:1] * steps)
    sine, cosine = sine * damp, cosine * damp
    power = jnp.where(lax.broadcasted_iota(jnp.int32, (GRID, LANES), 1) < HALF, 1.0, steps)
    for pair in range(2):
        c, s = power * cosine, power * sine
        for at, value in enumerate((
            jnp.concatenate([c, s], axis=0), jnp.concatenate([s, -c], axis=0)
        )):
            high, low = split(value)
            cols = slice((2 * at + pair) * LANES, (2 * at + pair + 1) * LANES)
            left_ref[0, :, cols] = high
            left_ref[1, :, cols] = low
        power = power * (steps * steps)
    sine, cosine = sincos(flat[1:2] * steps)
    siny_ref[...] = sine * damp
    cosy_ref[...] = cosine * damp
    planes = grid_ref.shape[0] // GRID
    depth = sinz_ref.shape[0]
    deep = signed_steps(g * planes + lax.broadcasted_iota(jnp.int32, (depth, LANES), 0))
    sine, cosine = sincos(flat[2:3] * deep)
    damp = jnp.exp(-spread * (deep * deep))
    sinz_ref[...] = sine * damp
    cosz_ref[...] = cosine * damp

    for turn in turns[:-1]:
        to = lax.rem(k + turn, ka)
        value = rows_ref[:, to, b]
        for step in range(1, ba):
            copies1[turn, step].wait_recv()
            value = value + first[step - 1, turn]
        held[turn - 1] = value
        copy = pltpu.make_async_remote_copy(
            src_ref=held.at[turn - 1],
            dst_ref=second.at[turn - 1],
            send_sem=send2.at[turn - 1],
            recv_sem=recv2.at[turn - 1],
            device_id={"ka": to},
            device_id_type=mesh_id,
        )
        copy.start()
        copies2[turn] = copy

    line = steps[:, :1]

    def plane(z, carry, along):
        sums = list(carry)
        cz, sz = cosz_ref[pl.ds(z, 1), :], sinz_ref[pl.ds(z, 1), :]
        cy, sy = cosy_ref[...], siny_ref[...]
        cosine = cz * cy - sz * sy
        sine = sz * cy + cz * sy
        index = g * planes + z
        height = grid_step * jnp.where(index >= GRID // 2, index - GRID, index).astype(jnp.float32)
        at = 0
        for pair in range(2):
            wave = along[:, pair * LANES:(pair + 1) * LANES] * cosine
            wave = wave - along[:, (2 + pair) * LANES:(3 + pair) * LANES] * sine
            for j in range(4 - 2 * pair):
                part = jnp.sum(wave.reshape(GRID // SUB, SUB, LANES), axis=0)
                for _ in range(4 - 2 * pair - j):
                    sums[at] = sums[at] + part
                    part = part * height
                    at += 1
                wave = wave * line
        return tuple(sums)

    def body(chunk, carry):
        start = pl.multiple_of(chunk * CHUNK * GRID, GRID)
        high, low = split(grid_ref[pl.ds(start, CHUNK * GRID), :])
        along = mdot(high, left_ref[0]) + mdot(low, left_ref[0]) + mdot(high, left_ref[1])
        for turn in range(CHUNK):
            carry = plane(chunk * CHUNK + turn, carry, along[turn * GRID:(turn + 1) * GRID])
        return carry

    zero = jnp.zeros((SUB, LANES), jnp.float32)
    sums = lax.fori_loop(0, planes // CHUNK, body, (zero,) * 13)
    rows = {}
    at = 0
    for pair in range(2):
        for j in range(4 - 2 * pair):
            for l in range(4 - 2 * pair - j):
                value = jnp.sum(sums[at], axis=0, keepdims=True)
                at += 1
                rows[2 * pair, j, l] = value
                if 2 * pair + 1 + j + l <= 3:
                    rows[2 * pair + 1, j, l] = pltpu.roll(value, HALF, 1)
    pieces = [rows[power] for power in POWERS]
    mono = jnp.concatenate(pieces + [jnp.zeros((ROWS - len(pieces), LANES), jnp.float32)], axis=0)
    sent[...] = mono
    for step in range(1, ga):
        peer = lax.rem(g + step, ga)
        copy = pltpu.make_async_remote_copy(
            src_ref=sent,
            dst_ref=third.at[step - 1],
            send_sem=send3.at[step - 1],
            recv_sem=recv3.at[step - 1],
            device_id={"ga": peer},
            device_id_type=mesh_id,
        )
        copy.start()
        copies3[step] = copy

    value = rows_ref[:, k, b]
    for step in range(1, ba):
        copies1[0, step].wait_recv()
        value = value + first[step - 1, 0]
    for turn in turns[:-1][::-1]:
        copies2[turn].wait_recv()
        value = value + second[turn - 1]
    total_ref[...] = value
    for step in range(1, ga):
        copies3[step].wait_recv()
        mono = mono + third[step - 1]
    row = lax.broadcasted_iota(jnp.int32, (ROWS, LANES), 0)
    mono = jnp.where(row == KIND_ROW, kinds, mono)
    mine = mono
    for block in range(1, blocks):
        mine = jnp.where(g == block, pltpu.roll(mono, LANES - block * per, 1), mine)
    terms_ref[...] = mine
    for copy in [*copies1.values(), *copies2.values(), *copies3.values()]:
        copy.wait_send()


def finish(rows, owner_map, species, positions, widths, grid):
    spins, ka, ba, per, pad = rows.shape
    ga = lax.axis_size("ga")
    planes = grid.shape[0] // GRID
    chunk = (spins, per, pad)
    vmem = pl.BlockSpec(memory_space=pltpu.VMEM)
    smem = pl.BlockSpec(memory_space=pltpu.SMEM)
    return pl.pallas_call(
        finish_kernel,
        out_shape=(
            jax.ShapeDtypeStruct(chunk, jnp.float32),
            jax.ShapeDtypeStruct((ROWS, LANES), jnp.float32),
        ),
        in_specs=[smem] + [vmem] * 5,
        out_specs=(vmem, vmem),
        scratch_shapes=[
            pltpu.VMEM((ba - 1, ka, *chunk), jnp.float32),
            pltpu.VMEM((ka - 1, *chunk), jnp.float32),
            pltpu.VMEM((ka - 1, *chunk), jnp.float32),
            pltpu.VMEM((ROWS, LANES), jnp.float32),
            pltpu.VMEM((ga - 1, ROWS, LANES), jnp.float32),
            pltpu.VMEM((2, 2 * GRID, 4 * LANES), jnp.bfloat16),
            pltpu.VMEM((GRID, LANES), jnp.float32),
            pltpu.VMEM((GRID, LANES), jnp.float32),
            pltpu.VMEM((-(-planes // SUB) * SUB, LANES), jnp.float32),
            pltpu.VMEM((-(-planes // SUB) * SUB, LANES), jnp.float32),
            pltpu.SemaphoreType.DMA((ba - 1, ka)),
            pltpu.SemaphoreType.DMA((ba - 1, ka)),
            pltpu.SemaphoreType.DMA((ka - 1,)),
            pltpu.SemaphoreType.DMA((ka - 1,)),
            pltpu.SemaphoreType.DMA((ga - 1,)),
            pltpu.SemaphoreType.DMA((ga - 1,)),
        ],
        compiler_params=pltpu.CompilerParams(collective_id=0, has_side_effects=True),
    )(widths, rows, owner_map, species, positions, grid)


def tail_kernel(total_ref, terms_ref, multipole_ref, open_ref, density_ref, force_ref):
    spins, parts, per, entries = density_ref.shape
    high, low = split(total_ref[...])
    whole = mdot(high, open_ref[...]) + mdot(low, open_ref[...])
    real = None
    for s in range(spins):
        rows = slice(s * per, (s + 1) * per)
        density_ref[s, 0] = whole[rows, :entries]
        density_ref[s, 1] = whole[rows, PAD:PAD + entries]
        real = whole[rows, :entries] if real is None else real + whole[rows, :entries]
    moments = lax.dot_general(
        multipole_ref[...], real, (((1,), (1,)), ((), ())), precision=highest,
        preferred_element_type=jnp.float32,
    )
    kinds = terms_ref[KIND_ROW:KIND_ROW + 1, :per]
    moments = jnp.where(kinds == 0.0, moments[:NL], moments[NL:])
    index = {power: at for at, power in enumerate(POWERS)}
    for c in range(3):
        force = None
        for l, shape in enumerate(SHAPES):
            term = None
            for power, factor in shape.items():
                at = index[tuple(p + (axis == c) for axis, p in enumerate(power))]
                part = terms_ref[at:at + 1, :per] * factor
                term = part if term is None else term + part
            term = term * moments[l:l + 1]
            force = term if force is None else force + term
        force_ref[c:c + 1, :] = force


def tail(total, terms, multipole):
    spins, per, pad = total.shape
    return pl.pallas_call(
        tail_kernel,
        out_shape=(
            jax.ShapeDtypeStruct((spins, 2, per, ENTRIES), jnp.float32),
            jax.ShapeDtypeStruct((3, per), jnp.float32),
        ),
    )(
        total.reshape(spins * per, pad), terms, multipole.reshape(SPECIES * NL, ENTRIES),
        jnp.asarray(open_table(), jnp.bfloat16),
    )


def shards(
    coefficients, occupied, kweights, owner_map, species, positions, multipole, widths, potential
):
    spins = coefficients.shape[0]
    ka, ba = lax.axis_size("ka"), lax.axis_size("ba")
    owner_map = owner_map.reshape(1, -1)
    rows = gram(coefficients, occupied, kweights, owner_map)
    rows = rows.reshape(spins, ka, ba, -1, PAD)
    grid = potential.reshape(2, -1, GRID)
    grid = jnp.concatenate([grid[1], grid[0]], axis=1)
    total, terms = finish(rows, owner_map, species.reshape(1, -1), positions, widths, grid)
    return tail(total, terms, multipole)


def solution(mesh):
    placed = (
        P(None, None, ("grp", "ka"), "ba", "ga"),
        P(None, ("grp", "ka")),
        P(("grp", "ka")),
        P("grp"),
        P("grp"),
        P(None, "grp"),
        P(),
        P(),
        P(None, ("grp", "ga")),
    )
    return jax.shard_map(
        shards,
        mesh=mesh,
        in_specs=placed,
        out_specs=(
            P(None, None, ("grp", "ka", "ga", "ba"), None),
            P(None, ("grp", "ka", "ga", "ba")),
        ),
        check_vma=False,
    )
```

time: 94.6 us -> 43.2 us (0.46)
  the two profiles are of different devices: /device:TPU:15 before, /device:TPU:0 now
where the time goes in v1:
time: 43.2 us; the launch traced here: 43 us
  Pallas kernels  34.9 us (81%)
  local copies, waits for them, and re-layouts  5.97 us (14%)
  other arithmetic  1.4 us (3%)
  between operations  0.73 us (2%)
    pallas_call x1, Pallas kernels, finish(): pl.pallas_call(finish_kernel, out_shape=(jax.ShapeDtypeStruct(chunk, jnp....  17.7 us
    pallas_call x1, Pallas kernels, gram(): pl.pallas_call(gram_kernel, out_shape=jax.ShapeDtypeStruct((spins, atoms,...  14.9 us
    slice x1, local copies, waits for them, and re-layouts, shards(): grid = jnp.concatenate([grid[1], grid[0]], axis=1)  4 us
    pallas_call x1, Pallas kernels, tail(): pl.pallas_call(tail_kernel, out_shape=(jax.ShapeDtypeStruct((spins, 2, pe...  2.28 us
    concatenate x1, other arithmetic, shards(): grid = jnp.concatenate([grid[1], grid[0]], axis=1)  1.4 us
    unnamed x13, local copies, waits for them, and re-layouts  0.97 us

profile of v1, /device:TPU:0, one launch (start us, length us, event | category | flops | bytes accessed | tf_op | source)
XLA Modules:
  0.0 43.0 jit_solution(4925456176761285648)
XLA Ops:
  0.6 4.0 %slice_reduce_fusion.1 = (f32[110592]{0:T(1024)S(1)}, f32[110592]{0:T(1024)S(1)}) fusion(f32[2,110592]{1,0:T(2,128)} %param.19), kind=kLoop, calls=%fused_computation.2 | loop fusion | bytes 1769472 | tf_op jit(solution)/shard_map/slice | solution.py:519
  4.6 0.2 squeeze.6
  4.8 0.2 squeeze.7
  5.0 0.0 copy-start.1
  5.0 0.0 copy-start.2
  5.1 0.0 copy-start.3
  5.1 0.0 copy-start.4
  5.1 1.4 %pad_maximum_fusion.grid_ref = f32[1152,192]{1,0:T(8,128)} fusion(f32[1152,96]{1,0:T(8,128)S(1)} %squeeze.7, f32[1152,96]{1,0:T(8,128)S(1)} %squeeze.6), kind=kLoop, calls=%fused_computation | loop fusion | flops 221184 | bytes 1769472 | tf_op jit(solution)/shard_map/concatenate | solution.py:519
  6.5 0.0 copy-done.1
  6.5 0.0 copy-done.2
  6.5 0.0 copy-done.3
  6.5 0.0 copy-done.4
  6.5 14.9 %shard_map.122 = f32[2,256,384]{2,1,0:T(8,128)S(1)} custom-call(s32[2,2]{1,0:T(2,128)S(1)} %copy-done.3, f32[2]{0:T(128)S(1)} %copy-done.4, bf16[2,2,2,256,4608]{4,3,2,1,0:T(8,128)(2,1)} %x_hbm.1, s32[1,512]{1,0:T(1,128)S(1)} %bitcast.6, bf16[384,384]{1,0:T(8,128)(2,1)S(1)} %copy-done.1), custom_call_target="tpu_custom_call" | custom-call | tf_op jit(solution)/shard_map/pallas_call | solution.py:208
  21.4 0.0 copy-start
  21.4 0.9 %copy-done = f32[2,256,384]{2,1,0:T(8,128)} copy-done((f32[2,256,384]{2,1,0:T(8,128)}, f32[2,256,384]{2,1,0:T(8,128)S(1)}, u32[]{:S(2)}) %copy-start) | copy-done | bytes 786456
  22.3 0.0 copy-start.5
  22.3 17.7 %shard_map.123 = (f32[2,32,384]{2,1,0:T(8,128)}, f32[24,128]{1,0:T(8,128)}) custom-call(f32[2]{0:T(128)} %width_ref.1, f32[2,4,2,32,384]{4,3,2,1,0:T(8,128)} %bitcast.4, s32[1,512]{1,0:T(1,128)} %bitcast.5, s32[1,512]{1,0:T(1,128)} %bitcast.8, f32[3,512]{1,0:T(4,128)} %place_ref.1, f32[1152,192]{1,0:T(8,128)} %pad_maximum_fusion.grid_ref), custom_call_target="tpu_custom_call" | custom-call | tf_op jit(solution)/shard_map/pallas_call | solution.py:436
  40.1 0.0 copy-done.5
  40.1 0.6 %reshape.28.multipole_ref = f32[18,324]{1,0:T(8,128)} reshape(f32[2,9,324]{2,1,0:T(8,128)S(1)} %copy.14) | data formatting | bytes 46656 | tf_op jit(solution)/shard_map/reshape | solution.py:505
  40.7 2.3 %shard_map.124 = (f32[2,2,32,324]{3,2,1,0:T(8,128)}, f32[3,32]{1,0:T(4,128)}) custom-call(f32[64,384]{1,0:T(8,128)} %bitcast.7, f32[24,128]{1,0:T(8,128)} %get-tuple-element.5.terms_ref, f32[18,324]{1,0:T(8,128)} %reshape.28.multipole_ref, bf16[384,768]{1,0:T(8,128)(2,1)} %constant.5.clone.open_ref), custom_call_target="tpu_custom_call" | custom-call | tf_op jit(solution)/shard_map/pallas_call | solution.py:498
  (1 shorter events, 0.0 us)
Async XLA Ops:
  5.0 1.4 %copy-start.1 = (bf16[384,384]{1,0:T(8,128)(2,1)S(1)}, bf16[384,384]{1,0:T(8,128)(2,1)}, u32[]{:S(2)}) copy-start(bf16[384,384]{1,0:T(8,128)(2,1)} %constant.4.clone.fold_ref) | copy-start | bytes 884740
  5.0 1.4 %copy-start.2 = (s32[512]{0:T(512)S(1)}, s32[512]{0:T(512)}, u32[]{:S(2)}) copy-start(s32[512]{0:T(512)} %param.14) | copy-start | bytes 6148
  5.1 1.4 %copy-start.3 = (s32[2,2]{1,0:T(2,128)S(1)}, s32[2,2]{1,0:T(2,128)}, u32[]{:S(2)}) copy-start(s32[2,2]{1,0:T(2,128)} %occ_ref.1) | copy-start | bytes 52
  5.1 1.4 %copy-start.4 = (f32[2]{0:T(128)S(1)}, f32[2]{0:T(128)}, u32[]{:S(2)}) copy-start(f32[2]{0:T(128)} %weight_ref.1) | copy-start | bytes 28
  21.4 0.9 %copy-start = (f32[2,256,384]{2,1,0:T(8,128)}, f32[2,256,384]{2,1,0:T(8,128)S(1)}, u32[]{:S(2)}) copy-start(f32[2,256,384]{2,1,0:T(8,128)S(1)} %shard_map.122) | copy-start | bytes 2359300
  22.3 17.7 %copy-start.5 = (f32[2,9,324]{2,0,1:T(2,128)S(1)}, f32[2,9,324]{2,0,1:T(2,128)}, u32[]{:S(2)}) copy-start(f32[2,9,324]{2,0,1:T(2,128)} %param.17) | copy-start | bytes 69988

commit v2 on v1

v2 whole, which is shorter than its diff:
```python
import functools
import math

import jax
import jax.numpy as jnp
import numpy as np
from jax import lax
from jax.experimental import pallas as pl
from jax.experimental.pallas import tpu as pltpu
from jax.sharding import PartitionSpec as P

NPROJ = 18
SPECIES = 2
NL = 9
GRID = 96
LANES = 128
SUB = 8
ENTRIES = NPROJ * NPROJ
PAD = -(-ENTRIES // LANES) * LANES
WIN = SUB * NPROJ
SLOTS = 2
HALF = LANES // 2
CHUNK = 3
FOLD = 4

grid_step = 0.0625
highest = lax.Precision.HIGHEST


def group_width():
    return NPROJ * LANES // math.gcd(NPROJ, LANES)


@functools.lru_cache(None)
def fold_table():
    q = np.zeros((PAD, PAD), np.float32)
    for i in range(NPROJ):
        for j in range(i):
            q[i * NPROJ + j, i * NPROJ + j] += 1.0
            q[j * NPROJ + i, i * NPROJ + j] -= 1.0
    return q


@functools.lru_cache(None)
def open_table():
    u = np.zeros((PAD, 2 * PAD), np.float32)
    for i in range(NPROJ):
        for j in range(NPROJ):
            u[min(i, j) * NPROJ + max(i, j), i * NPROJ + j] = 1.0
            if i > j:
                u[i * NPROJ + j, PAD + i * NPROJ + j] = 1.0
            elif i < j:
                u[j * NPROJ + i, PAD + i * NPROJ + j] = -1.0
    return u


POWERS = [(i, j, k) for i in range(4) for j in range(4 - i) for k in range(4 - i - j)]
SHAPES = [
    {(0, 0, 0): 1.0},
    {(1, 0, 0): 1.0},
    {(0, 1, 0): 1.0},
    {(0, 0, 1): 1.0},
    {(1, 1, 0): 1.0},
    {(0, 1, 1): 1.0},
    {(1, 0, 1): 1.0},
    {(2, 0, 0): 1.0, (0, 2, 0): -1.0},
    {(0, 0, 2): 2.0, (2, 0, 0): -1.0, (0, 2, 0): -1.0},
]
KIND_ROW = len(POWERS)
ROWS = -(-(KIND_ROW + 1) // SUB) * SUB


def split(value):
    high = value.astype(jnp.bfloat16)
    return high, (value - high.astype(jnp.float32)).astype(jnp.bfloat16)


def mdot(a, b):
    return jnp.dot(a, b, preferred_element_type=jnp.float32)


def flags(value):
    return value.astype(jnp.float32).astype(jnp.bfloat16)


def before(count):
    row = lax.broadcasted_iota(jnp.int32, (count, count), 0)
    col = lax.broadcasted_iota(jnp.int32, (count, count), 1)
    return flags(row < col)


def sincos(angle):
    turns = jnp.floor(angle * (2.0 / math.pi) + 0.5)
    rest = ((angle - turns * 1.5703125) - turns * 4.837512969970703125e-4) - turns * 7.54978995489188216e-8
    z = rest * rest
    sine = ((-1.9515295891e-4 * z + 8.3321608736e-3) * z - 1.6666654611e-1) * z * rest + rest
    cosine = (
        (2.443315711809948e-5 * z - 1.388731625493765e-3) * z + 4.166664568298827e-2
    ) * z * z - 0.5 * z + 1.0
    quarter = turns.astype(jnp.int32) & 3
    odd = (quarter & 1) == 1
    s = jnp.where(odd, cosine, sine)
    c = jnp.where(odd, sine, cosine)
    return jnp.where(quarter >= 2, -s, s), jnp.where((quarter == 1) | (quarter == 2), -c, c)


def signed_steps(index):
    return grid_step * jnp.where(index >= GRID // 2, index - GRID, index).astype(jnp.float32)


def main_kernel(
    occ_ref, weight_ref, width_ref, x_hbm, wave_hbm, fold_hbm, open_hbm, owner_ref, kind_ref,
    place_ref, multipole_ref, density_ref, force_ref,
    x_ref, xa_ref, xb_ref, sc_ref, t_ref, route_ref, rows_ref, first, held, second, sent, third,
    wave_ref, fold_ref, open_ref, left_ref, cosy_ref, siny_ref, cosz_ref, sinz_ref,
    sems, loads, send1, recv1, send2, recv2, send3, recv3,
):
    mesh_id = pl.DeviceIdType.MESH
    ka, ba, ga = (lax.axis_size(name) for name in ("ka", "ba", "ga"))
    k, b, g = (lax.axis_index(name) for name in ("ka", "ba", "ga"))
    spins, groups, _, kcount, bcount, width = x_ref.shape
    atoms = t_ref.shape[1]
    per = rows_ref.shape[3]
    blocks = ga
    owners = ka * ba
    group_atoms = width // NPROJ
    total = spins * groups

    def fetch(n):
        s, group = n // groups, n % groups
        cols = pl.ds(pl.multiple_of(group * width, width), width)
        return pltpu.make_async_copy(
            x_hbm.at[s, :, :, :, cols], x_ref.at[s, group], sems.at[s, group]
        )

    others = [
        pltpu.make_async_copy(source, target, loads.at[at])
        for at, (source, target) in enumerate((
            (fold_hbm, fold_ref), (wave_hbm, wave_ref), (open_hbm, open_ref)
        ))
    ]
    fetch(0).start()
    for n in range(1, total):
        fetch(n).start()
        if n == 1:
            for copy in others:
                copy.start()
    barrier = pltpu.get_barrier_semaphore()
    for name, me, size in (("ka", k, ka), ("ba", b, ba), ("ga", g, ga)):
        for step in range(1, size):
            pl.semaphore_signal(
                barrier, inc=1, device_id={name: lax.rem(me + step, size)}, device_id_type=mesh_id
            )

    owner = owner_ref[:, :atoms]
    for block in range(1, blocks):
        piece = owner_ref[:, block * atoms:(block + 1) * atoms]
        owner = jnp.where(g == block, piece, owner)
    lower = before(atoms)
    member = lax.broadcasted_iota(jnp.int32, (max(owners, 2 * SUB), atoms), 0) == owner
    count = mdot(flags(member), lower)
    rank = jnp.sum(jnp.where(member, count, 0.0), axis=0, keepdims=True)
    spot = owner.astype(jnp.float32) * per + rank
    place = lax.broadcasted_iota(jnp.int32, (atoms, atoms), 0).astype(jnp.float32)
    route_ref[...] = flags(place == spot)

    columns = []
    for block in range(blocks):
        span = slice(block * atoms, (block + 1) * atoms)
        mine = owner_ref[:, span] == k * ba + b
        rank = mdot(jnp.broadcast_to(flags(mine), (2 * SUB, atoms)), lower)[:1]
        spot = lax.broadcasted_iota(jnp.int32, (per, atoms), 0).astype(jnp.float32)
        chosen = mine & (rank == spot)
        columns.append([
            jnp.sum(jnp.where(chosen, value, 0.0), axis=1, keepdims=True)
            for value in (
                place_ref[0:1, span], place_ref[1:2, span], place_ref[2:3, span],
                kind_ref[:, span].astype(jnp.float32),
            )
        ])
    index = lax.broadcasted_iota(jnp.int32, (HALF, LANES), 1)
    table = jnp.zeros((HALF, LANES), jnp.float32)
    spare = HALF - blocks * per
    for at in range(4):
        pieces = [columns[block][at] for block in range(blocks)]
        if spare:
            pieces.append(jnp.zeros((spare, 1), jnp.float32))
        table = jnp.where(index == at, jnp.concatenate(pieces, axis=0), table)
    flat = jnp.concatenate([table, table], axis=0).T
    kinds = flat[3:4]
    spread = jnp.where(kinds == 0.0, width_ref[0], width_ref[1])

    steps = signed_steps(lax.broadcasted_iota(jnp.int32, (GRID, LANES), 0))
    damp = jnp.exp(-spread * (steps * steps))
    sine, cosine = sincos(flat[0:1] * steps)
    sine, cosine = sine * damp, cosine * damp
    power = jnp.where(lax.broadcasted_iota(jnp.int32, (GRID, LANES), 1) < HALF, 1.0, steps)
    gap = jnp.zeros((LANES - GRID, LANES), jnp.float32)
    for pair in range(2):
        c, s = power * cosine, power * sine
        for at, pieces in enumerate(((c, gap, s, gap), (s, gap, -c, gap))):
            high, low = split(jnp.concatenate(pieces, axis=0))
            cols = slice((2 * at + pair) * LANES, (2 * at + pair + 1) * LANES)
            left_ref[0, :, cols] = high
            left_ref[1, :, cols] = low
        power = power * (steps * steps)
    number = lax.broadcasted_iota(jnp.int32, (GRID, LANES), 0)
    line = signed_steps(FOLD * (number % (GRID // FOLD)) + number // (GRID // FOLD))
    damp = jnp.exp(-spread * (line * line))
    sine, cosine = sincos(flat[1:2] * line)
    siny_ref[...] = sine * damp
    cosy_ref[...] = cosine * damp
    planes = wave_ref.shape[0] * LANES // (2 * GRID * GRID)
    depth = sinz_ref.shape[0]
    deep = signed_steps(g * planes + lax.broadcasted_iota(jnp.int32, (depth, LANES), 0))
    sine, cosine = sincos(flat[2:3] * deep)
    damp = jnp.exp(-spread * (deep * deep))
    sinz_ref[...] = sine * damp
    cosz_ref[...] = cosine * damp

    band = lax.broadcasted_iota(jnp.int32, (LANES, bcount), 1) + b * bcount
    lane = lax.broadcasted_iota(jnp.int32, (SUB, LANES), 1)
    row = lax.broadcasted_iota(jnp.int32, (SUB, LANES), 0)
    shifts = [NPROJ * row + (at * LANES + lane) % NPROJ for at in range(PAD // LANES)]
    past = lax.broadcasted_iota(jnp.int32, (WIN, LANES), 1) - lax.broadcasted_iota(
        jnp.int32, (WIN, LANES), 0) // NPROJ * NPROJ

    def turn(n, xt_ref, t):
        s, group = n // groups, n % groups
        cols = slice(t*LANES, (t+1)*LANES)
        for k in range(kcount):
            mask = (band < occ_ref[s, k]).astype(jnp.float32).astype(jnp.bfloat16)
            for c in range(2):
                v = x_ref[s, group, c, k, :, cols].T * mask
                at = t*LANES
                while at < (t+1)*LANES:
                    w = at // WIN
                    end = min((w+1)*WIN, (t+1)*LANES)
                    xt_ref[k, w, (1 - c) * WIN + at - w*WIN:(1 - c) * WIN + end - w*WIN, :] = v[at - t*LANES:end - t*LANES]
                    at = end

    def window(n, xt_ref, w):
        s, group = n // groups, n % groups
        base = (w*WIN)//LANES*LANES
        o = w*WIN - base
        win = slice(base, base + 2*LANES)
        take = past < o + NPROJ - LANES
        re = im = None
        for k in range(kcount):
            both = mdot(xt_ref[k, w], x_ref[s, group, 1, k, :, win])
            r = mdot(xt_ref[k, w, WIN:], x_ref[s, group, 0, k, :, win]) + both[:WIN]
            m = both[WIN:]
            weight = weight_ref[k]
            r = jnp.where(take, r[:, LANES:], r[:, :LANES]) * weight
            m = jnp.where(take, m[:, LANES:], m[:, :LANES]) * weight
            re = r if re is None else re + r
            im = m if im is None else im + m
        sc_ref[w % SLOTS, 0] = re
        sc_ref[w % SLOTS, 1] = im

    def unfold(n, w):
        s, group = n // groups, n % groups
        o = w*WIN % LANES
        lifts = [(o + shift) & (LANES - 1) for shift in shifts]
        for c in range(2):
            tiles = [None]*(PAD//LANES)
            for i in range(NPROJ):
                piece = sc_ref[w % SLOTS, c, pl.ds(i, SUB, stride=NPROJ), :]
                for at in range(i*NPROJ // LANES, (i*NPROJ + NPROJ - 1) // LANES + 1):
                    part = jnp.take_along_axis(piece, lifts[at], axis=1, mode="promise_in_bounds")
                    tiles[at] = part if tiles[at] is None else jnp.where(lane >= i*NPROJ - at*LANES, part, tiles[at])
            for at, v in enumerate(tiles):
                here = pl.multiple_of(group * group_atoms + w * SUB, SUB)
                t_ref[c, pl.ds(here, SUB), at*LANES:(at+1)*LANES] = v

    def step(n, here, there):
        after = jnp.minimum(n + 1, total - 1)

        @pl.when(n + 1 < total)
        def _():
            fetch(n + 1).wait()

        for w in range(width // WIN):
            window(n, here, w)
            turn(after, there, w)
            if w == 0:
                turn(after, there, width // LANES - 1)
            unfold(n, w)

    entry = lax.broadcasted_iota(jnp.int32, (atoms, PAD), 1)
    keep = (entry // NPROJ <= entry % NPROJ) & (entry < ENTRIES)

    def pack(s):
        fold = fold_ref[...]
        high, low = split(jnp.where(entry < ENTRIES, t_ref[1], 0.0))
        packed = jnp.where(keep, t_ref[0], 0.0) + (mdot(high, fold) + mdot(low, fold))
        high, low = split(packed)
        routed = mdot(route_ref[...], high) + mdot(route_ref[...], low)
        for o in range(owners):
            rows_ref[s, o // ba, o % ba] = routed[o * per:(o + 1) * per]

    turns = [t // 2 + 1 if t % 2 == 0 else ka - 1 - t // 2 for t in range(ka - 1)][::-1]

    def swap(s, turn, step):
        peer = lax.rem(b + step, ba)
        return pltpu.make_async_remote_copy(
            src_ref=rows_ref.at[s, lax.rem(k + turn, ka), peer],
            dst_ref=first.at[s, step - 1, turn],
            send_sem=send1.at[s, step - 1, turn],
            recv_sem=recv1.at[s, step - 1, turn],
            device_id={"ba": peer},
            device_id_type=mesh_id,
        )

    def hop(s, turn):
        return pltpu.make_async_remote_copy(
            src_ref=held.at[s, turn - 1],
            dst_ref=second.at[s, turn - 1],
            send_sem=send2.at[s, turn - 1],
            recv_sem=recv2.at[s, turn - 1],
            device_id={"ka": lax.rem(k + turn, ka)},
            device_id_type=mesh_id,
        )

    def share(step):
        return pltpu.make_async_remote_copy(
            src_ref=sent,
            dst_ref=third.at[step - 1],
            send_sem=send3.at[step - 1],
            recv_sem=recv3.at[step - 1],
            device_id={"ga": lax.rem(g + step, ga)},
            device_id_type=mesh_id,
        )

    def start_swaps(s):
        for turn in turns + [0]:
            for step in range(1, ba):
                swap(s, turn, step).start()

    def chip_sum(s, turn):
        value = rows_ref[s, lax.rem(k + turn, ka), b]
        for step in range(1, ba):
            swap(s, turn, step).wait_recv()
            value = value + first[s, step - 1, turn]
        return value

    def start_hops(s):
        for turn in turns:
            held[s, turn - 1] = chip_sum(s, turn)
            hop(s, turn).start()

    fetch(0).wait()
    for t in range(width // LANES):
        turn(0, xa_ref, t)
    for s in range(spins):
        if groups % 2 == 0:
            @pl.loop(s * groups // 2, (s + 1) * groups // 2)
            def _(pair):
                step(2 * pair, xa_ref, xb_ref)
                if s:
                    @pl.when(pair == s * groups // 2)
                    def _():
                        start_hops(s - 1)
                step(2 * pair + 1, xb_ref, xa_ref)
        else:
            for n in range(s * groups, (s + 1) * groups):
                step(n, *((xa_ref, xb_ref) if n % 2 == 0 else (xb_ref, xa_ref)))
                if s and n == s * groups:
                    start_hops(s - 1)
        if s == 0:
            others[0].wait()
            pl.semaphore_wait(barrier, ka + ba + ga - 3)
        pack(s)
        start_swaps(s)
    others[1].wait()

    def plane(z, carry, along):
        sums = list(carry)
        cz, sz = cosz_ref[pl.ds(z, 1), :], sinz_ref[pl.ds(z, 1), :]
        cy, sy = cosy_ref[...], siny_ref[...]
        cosine = cz * cy - sz * sy
        sine = sz * cy + cz * sy
        index = g * planes + z
        height = grid_step * jnp.where(index >= GRID // 2, index - GRID, index).astype(jnp.float32)
        at = 0
        for pair in range(2):
            wave = along[:, pair * LANES:(pair + 1) * LANES] * cosine
            wave = wave - along[:, (2 + pair) * LANES:(3 + pair) * LANES] * sine
            for j in range(4 - 2 * pair):
                part = jnp.sum(wave.reshape(GRID // SUB, SUB, LANES), axis=0)
                for _ in range(4 - 2 * pair - j):
                    sums[at] = sums[at] + part
                    part = part * height
                    at += 1
                wave = wave * line
        return tuple(sums)

    lanes = lax.broadcasted_iota(jnp.int32, (GRID // FOLD, LANES), 1)

    def rows_of(z, c):
        start = z * (2 * GRID * GRID // LANES) + c
        one, two, three = (
            wave_ref[pl.ds(start + 2 * j, GRID // FOLD, stride=2 * (FOLD - 1)), :]
            for j in range(FOLD - 1)
        )
        return jnp.concatenate([
            one,
            pltpu.roll(jnp.where(lanes >= 96, one, two), 32, 1),
            pltpu.roll(jnp.where(lanes >= 64, two, three), 64, 1),
            pltpu.roll(three, 96, 1),
        ], axis=0)

    def body(chunk, carry):
        value = jnp.concatenate([
            jnp.concatenate([rows_of(chunk * CHUNK + turn, c) for turn in range(CHUNK)], axis=0)
            for c in (1, 0)
        ], axis=1)
        high, low = split(value)
        along = mdot(high, left_ref[0]) + mdot(low, left_ref[0]) + mdot(high, left_ref[1])
        for turn in range(CHUNK):
            carry = plane(chunk * CHUNK + turn, carry, along[turn * GRID:(turn + 1) * GRID])
        return carry

    sums = (jnp.zeros((SUB, LANES), jnp.float32),) * 13
    sums = lax.fori_loop(0, 1, body, sums)
    start_hops(spins - 1)
    sums = lax.fori_loop(1, planes // CHUNK, body, sums)
    found = {}
    at = 0
    for pair in range(2):
        for j in range(4 - 2 * pair):
            for l in range(4 - 2 * pair - j):
                value = jnp.sum(sums[at], axis=0, keepdims=True)
                at += 1
                found[2 * pair, j, l] = value
                if 2 * pair + 1 + j + l <= 3:
                    found[2 * pair + 1, j, l] = pltpu.roll(value, HALF, 1)
    pieces = [found[power] for power in POWERS]
    mono = jnp.concatenate(pieces + [jnp.zeros((ROWS - len(pieces), LANES), jnp.float32)], axis=0)
    sent[...] = mono
    for step in range(1, ga):
        share(step).start()
    others[2].wait()
    real = None
    for s in range(spins):
        value = chip_sum(s, 0)
        for turn in turns[::-1]:
            hop(s, turn).wait_recv()
            value = value + second[s, turn - 1]
        high, low = split(value)
        whole = mdot(high, open_ref[...]) + mdot(low, open_ref[...])
        density_ref[s, 0] = whole[:, :ENTRIES]
        density_ref[s, 1] = whole[:, PAD:PAD + ENTRIES]
        real = whole[:, :ENTRIES] if real is None else real + whole[:, :ENTRIES]
    moments = lax.dot_general(
        multipole_ref[...], real, (((1,), (1,)), ((), ())), precision=highest,
        preferred_element_type=jnp.float32,
    )
    for step in range(1, ga):
        share(step).wait_recv()
        mono = mono + third[step - 1]
    mono = jnp.where(lax.broadcasted_iota(jnp.int32, (ROWS, LANES), 0) == KIND_ROW, kinds, mono)
    mine = mono
    for block in range(1, blocks):
        mine = jnp.where(g == block, pltpu.roll(mono, LANES - block * per, 1), mine)
    mine = mine[:, :per]
    moments = jnp.where(mine[KIND_ROW:KIND_ROW + 1] == 0.0, moments[:NL], moments[NL:])
    for c in range(3):
        force = None
        for l, shape in enumerate(SHAPES):
            term = None
            for power, factor in shape.items():
                at = POWERS.index(tuple(p + (axis == c) for axis, p in enumerate(power)))
                part = mine[at:at + 1] * factor
                term = part if term is None else term + part
            term = term * moments[l:l + 1]
            force = term if force is None else force + term
        force_ref[c:c + 1, :] = force
    for s in range(spins):
        for turn in turns + [0]:
            for step in range(1, ba):
                swap(s, turn, step).wait_send()
        for turn in turns:
            hop(s, turn).wait_send()
    for step in range(1, ga):
        share(step).wait_send()


def shards(
    coefficients, occupied, kweights, owner_map, species, positions, multipole, widths, potential
):
    spins, parts, kcount, bcount, columns = coefficients.shape
    ka, ba, ga = (lax.axis_size(name) for name in ("ka", "ba", "ga"))
    width = group_width()
    groups = columns // width
    atoms = columns // NPROJ
    per = atoms // (ka * ba)
    planes = potential.shape[1] // (GRID * GRID)
    deep = -(-planes // SUB) * SUB
    wave = potential.reshape(2, -1, LANES).transpose(1, 0, 2).reshape(-1, LANES)
    vmem = pl.BlockSpec(memory_space=pltpu.VMEM)
    smem = pl.BlockSpec(memory_space=pltpu.SMEM)
    hbm = pl.BlockSpec(memory_space=pl.ANY)
    f32, bf16 = jnp.float32, jnp.bfloat16
    dma = pltpu.SemaphoreType.DMA
    return pl.pallas_call(
        main_kernel,
        out_shape=(
            jax.ShapeDtypeStruct((spins, parts, per, ENTRIES), f32),
            jax.ShapeDtypeStruct((3, per), f32),
        ),
        in_specs=[smem] * 3 + [hbm] * 4 + [vmem] * 4,
        out_specs=(vmem, vmem),
        scratch_shapes=[
            pltpu.VMEM((spins, groups, parts, kcount, bcount, width), bf16),
            *[pltpu.VMEM((kcount, width // WIN, 2 * WIN, bcount), bf16)] * 2,
            pltpu.VMEM((SLOTS, 2, WIN, LANES), f32),
            pltpu.VMEM((2, atoms, PAD), f32),
            pltpu.VMEM((atoms, atoms), bf16),
            pltpu.VMEM((spins, ka, ba, per, PAD), f32),
            pltpu.VMEM((spins, ba - 1, ka, per, PAD), f32),
            pltpu.VMEM((spins, ka - 1, per, PAD), f32),
            pltpu.VMEM((spins, ka - 1, per, PAD), f32),
            pltpu.VMEM((ROWS, LANES), f32),
            pltpu.VMEM((ga - 1, ROWS, LANES), f32),
            pltpu.VMEM(wave.shape, f32),
            pltpu.VMEM((PAD, PAD), bf16),
            pltpu.VMEM((PAD, 2 * PAD), bf16),
            pltpu.VMEM((2, 2 * LANES, 4 * LANES), bf16),
            pltpu.VMEM((GRID, LANES), f32),
            pltpu.VMEM((GRID, LANES), f32),
            pltpu.VMEM((deep, LANES), f32),
            pltpu.VMEM((deep, LANES), f32),
            dma((spins, groups)),
            dma((3,)),
            dma((spins, ba - 1, ka)),
            dma((spins, ba - 1, ka)),
            dma((spins, ka - 1)),
            dma((spins, ka - 1)),
            dma((ga - 1,)),
            dma((ga - 1,)),
        ],
        compiler_params=pltpu.CompilerParams(
            collective_id=0, has_side_effects=True, vmem_limit_bytes=63 * 2**20
        ),
    )(
        occupied, kweights, widths, coefficients, wave,
        jnp.asarray(fold_table(), bf16), jnp.asarray(open_table(), bf16),
        owner_map.reshape(1, -1), species.reshape(1, -1), positions,
        multipole.reshape(SPECIES * NL, ENTRIES),
    )


def solution(mesh):
    placed = (
        P(None, None, ("grp", "ka"), "ba", "ga"),
        P(None, ("grp", "ka")),
        P(("grp", "ka")),
        P("grp"),
        P("grp"),
        P(None, "grp"),
        P(),
        P(),
        P(None, ("grp", "ga")),
    )
    return jax.shard_map(
        shards,
        mesh=mesh,
        in_specs=placed,
        out_specs=(
            P(None, None, ("grp", "ka", "ga", "ba"), None),
            P(None, ("grp", "ka", "ga", "ba")),
        ),
        check_vma=False,
    )
```

time: 43.2 us -> 32.5 us (0.75)
  Pallas kernels: 34.9 us -> 27.4 us
  local copies, waits for them, and re-layouts: 5.97 us -> 4.22 us
  other arithmetic: 1.4 us -> 0 us
    pallas_call x3 -> x1, Pallas kernels: 34.9 us -> 27.4 us  [shards(): pl.pallas_call(main_kernel, out_shape=(jax.ShapeDtypeStruct((spins, parts...]
    slice x1 -> x0, local copies, waits for them, and re-layouts: 4 us -> none  [shards(): grid = jnp.concatenate([grid[1], grid[0]], axis=1)]
    unnamed x13 -> x3, local copies, waits for them, and re-layouts: 0.97 us -> 3.6 us
    concatenate x1 -> x0, other arithmetic: 1.4 us -> none  [shards(): grid = jnp.concatenate([grid[1], grid[0]], axis=1)]
where the time goes in v2:
time: 32.5 us; the launch traced here: 32.2 us
  Pallas kernels  27.4 us (84%)
  local copies, waits for them, and re-layouts  4.22 us (13%)
  between operations  0.64 us (2%)
    pallas_call x1, Pallas kernels, shards(): pl.pallas_call(main_kernel, out_shape=(jax.ShapeDtypeStruct((spins, parts...  27.4 us
    unnamed x3, local copies, waits for them, and re-layouts  3.6 us

profile of v2, /device:TPU:0, one launch (start us, length us, event | category | flops | bytes accessed | tf_op | source)
XLA Modules:
  0.0 32.2 jit_solution(15870144542487041843)
XLA Ops:
  0.6 0.8 %copy.16 = f32[2,9,324]{2,1,0:T(8,128)S(1)} copy(f32[2,9,324]{2,0,1:T(2,128)} %param.17) | data formatting | bytes 46656 | tf_op args[6]
  1.4 0.6 %reshape.23.multipole_ref = f32[18,324]{1,0:T(8,128)} reshape(f32[2,9,324]{2,1,0:T(8,128)S(1)} %copy.16) | data formatting | bytes 46656 | tf_op jit(solution)/shard_map/reshape | solution.py:550
  2.0 27.4 %shard_map.122 = (f32[2,2,32,324]{3,2,1,0:T(8,128)}, f32[3,32]{1,0:T(4,128)}) custom-call(s32[2,2]{1,0:T(2,128)} %occ_ref.1, f32[2]{0:T(128)} %weight_ref.1, f32[2]{0:T(128)} %width_ref.1, bf16[2,2,2,256,4608]{4,3,2,1,0:T(8,128)(2,1)} %x_hbm.1, f32[1728,128]{1,0:T(8,128)} %bitcast.7, bf16[384,384]{1,0:T(8,128)(2,1)} %constant.4.clone.fold_hbm, ...), custom_call_target="tpu_custom_call" | custom-call | tf_op jit(solution)/shard_map/pallas_call | solution.py:506
  29.4 1.6 %copy.19 = f32[2,2,32,324]{3,2,1,0:T(8,128)} copy(f32[2,2,32,324]{3,2,1,0:T(8,128)} %get-tuple-element.4) | data formatting | bytes 331776
  31.0 1.2 %copy.20 = f32[3,32]{1,0:T(4,128)} copy(f32[3,32]{1,0:T(4,128)} %get-tuple-element.5) | data formatting | bytes 768
